TPU v7x, 32 devices: a whole 2x2x4 slice. The times are simulated.
32 devices in a mesh: prow: 8 (over y, x, core), pcol: 4 (over z).
Axes of the slice: x: 2, y: 2, z: 4, core: 2. Of those that a mesh axis runs over, the one named last changes fastest.
Arguments:
- u_window: float32 [6, 8, 512, 4, 4, 512], P(None, 'prow', None, None, 'pcol'), may hold values from -0.625 to 0.625
Outputs:
- lauum_columns: float32 [1024, 6, 8, 512], P('pcol', None, 'prow')
All inputs are finite; a program needn't handle non-finite values.
Results may differ from a plain program's by a relative error of at most 0.000061.
Values sent between devices are 32-bit elements; how exact they have to be, the bound alone decides.
No kernel may reach another device: no remote copies, remote signals or barrier semaphores. Data moves between devices by JAX's collectives and lax.ppermute only.
A program may use at most 192 MiB of HBM per device.

v0:
```python
import jax
import jax.numpy as jnp
from jax import lax
from jax.sharding import PartitionSpec as P


def broadcast(value, axis, source):
    kept = jnp.where(lax.axis_index(axis) == source, value, 0).astype(value.dtype)
    return lax.psum(kept, axis)


def contract(left, right):
    return lax.dot_general(
        left,
        right,
        (((1,), (1,)), ((), ())),
        precision=lax.Precision.HIGHEST,
        preferred_element_type=jnp.float32,
    )


def on_device(u_window):
    row_blocks = u_window.shape[0]
    block_size = u_window.shape[2]
    col_blocks = u_window.shape[3]
    prow_size = lax.axis_size("prow")
    pcol_size = lax.axis_size("pcol")
    my_row = lax.axis_index("prow")
    my_col = lax.axis_index("pcol")
    blocks = u_window.reshape(row_blocks * block_size, col_blocks * block_size)
    last_row = blocks[(row_blocks - 1) * block_size :]
    anchor = (row_blocks * prow_size - 2) * block_size
    row_ids = ((row_blocks - 1) * prow_size + my_row) * block_size + jnp.arange(
        block_size, dtype=jnp.int32
    )
    col_index = jnp.arange(col_blocks * block_size, dtype=jnp.int32)
    window_col = (
        col_index // block_size * pcol_size + my_col
    ) * block_size + col_index % block_size
    masked = jnp.where(
        row_ids[:, None] <= anchor + window_col[None, :], last_row, jnp.zeros_like(last_row)
    )
    first_panel = broadcast(masked, "prow", prow_size - 2)
    second_panel = broadcast(masked, "prow", prow_size - 1)
    panels = jnp.concatenate([first_panel, second_panel], 0)
    top_rows = blocks[: (row_blocks - 1) * block_size]
    ending = contract(panels, masked)
    summed = lax.psum_scatter(
        jnp.concatenate([contract(panels, top_rows), ending], 1),
        "pcol",
        scatter_dimension=0,
        tiled=True,
    )
    share_rows = summed.shape[0]
    return summed.reshape(share_rows, row_blocks, 1, block_size)


def solution(mesh):
    placed = (P(None, "prow", None, None, "pcol", None),)
    return jax.shard_map(
        on_device,
        mesh=mesh,
        in_specs=placed,
        out_specs=P("pcol", None, "prow", None),
        check_vma=False,
    )
```

profile of v0, /device:TPU:0, one launch (start us, length us, event | category | flops | bytes accessed | tf_op | source)
XLA Modules:
  0.0 495.6 jit_solution(5717784796368923473)
XLA Ops:
  6.5 0.0 all-reduce.3.cloned.1.call-start
  6.6 12.9 %slice_reduce_fusion.1 = f32[512,4,512]{2,1,0:T(4,128)S(1)} fusion(f32[6,1,512,4,1,512]{5,4,3,2,1,0:T(1,128)} %param.1), kind=kLoop, calls=%fused_computation.2 | loop fusion | bytes 8388608 | tf_op jit(solution)/shard_map/slice | solution.py:31
  19.4 2.0 copy.8
  21.4 0.0 copy-start
  21.4 4.3 fusion.1
  25.7 0.2 copy-done
  25.9 0.0 all-reduce.3.cloned.1.call-update
  26.0 0.2 reduce-scatter.2.cloned.1.call-start
  26.2 67.2 %slice_reduce_fusion = f32[5,512,4,512]{3,2,1,0:T(4,128)} fusion(f32[6,1,512,4,1,512]{5,4,3,2,1,0:T(1,128)} %param.1), kind=kLoop, calls=%fused_computation | loop fusion | bytes 41943040 | tf_op jit(solution)/shard_map/slice | solution.py:46
  93.4 21.0 %copy.9 = f32[320,8,4,512]{3,1,2,0:T(8,128)} copy(f32[320,8,4,512]{3,2,1,0:T(4,128)} %bitcast.9) | data formatting | bytes 41943040
  114.4 40.6 %all-reduce.3.cloned.1.call-done = (f32[512,2048]{1,0:T(8,128)}, f32[512,2048]{1,0:T(8,128)}) async-done(((f32[512,2048]{1,0:T(8,128)}, f32[512,2048]{1,0:T(8,128)}), (f32[512,2048]{1,0:T(8,128)}, f32[512,2048]{1,0:T(8,128)})) %all-reduce.3.cloned.1.call-update) | async-done | bytes 8388624 | tf_op jit(solution)/shard_map/psum | solution.py:9
  155.0 0.0 slice-start
  155.0 0.0 slice-start.1
  155.0 5.0 %constant_dynamic-update-slice_fusion.1 = f32[1024,2048]{1,0:T(8,128)} fusion(f32[512,2048]{1,0:T(8,128)} %get-tuple-element.5), kind=kLoop, calls=%fused_computation.27 | loop fusion | bytes 8388608
  160.0 0.0 copy-start.1
  160.0 0.0 slice-start.2
  160.0 5.2 %constant_dynamic-update-slice_fusion = f32[1024,2048]{1,0:T(8,128)} fusion(f32[1024,2048]{1,0:T(8,128)} %constant_dynamic-update-slice_fusion.1, f32[512,2048]{1,0:T(8,128)} %get-tuple-element.6), kind=kLoop, calls=%fused_computation.26 | loop fusion | bytes 8388608 | tf_op jit(solution)/shard_map/concatenate | solution.py:45
  165.2 0.0 copy-done.1
  165.2 0.0 slice-start.3
  165.2 0.0 slice-start.4
  165.2 18.1 %fusion = f32[1024,512]{1,0:T(8,128)} fusion(f32[1024,2048]{1,0:T(8,128)} %constant_dynamic-update-slice_fusion, f32[512,2048]{1,0:T(8,128)S(1)} %bitcast.14, s32[2048]{0:T(1024)S(1)} %fusion.16, s32[512]{0:T(512)S(1)} %iota_add_fusion), kind=kOutput, calls=%fused_computation.4 | convolution fusion | flops 12886999040 | bytes 14690304 | tf_op jit(solution)/shard_map/dot_general | solution.py:13
  183.3 0.0 slice-done
  183.3 0.0 slice-done.1
  183.3 0.0 slice-done.2
  183.3 0.0 slice-done.3
  183.3 0.0 slice-done.4
  183.3 75.4 %fusion.19 = f32[1024,2560]{1,0:T(8,128)} fusion(f32[1024,2048]{1,0:T(8,128)} %constant_dynamic-update-slice_fusion, f32[2560,2048]{1,0:T(8,128)S(1)} %bitcast.12), kind=kOutput, calls=%fused_computation.30 | convolution fusion | flops 64424509440 | bytes 39845888 | tf_op jit(solution)/shard_map/dot_general | solution.py:13
  258.7 10.2 %pad_maximum_fusion = f32[1024,3072]{1,0:T(8,128)} fusion(f32[1024,512]{1,0:T(8,128)} %fusion, f32[1024,2560]{1,0:T(8,128)} %fusion.19), kind=kLoop, calls=%fused_computation.1 | loop fusion | flops 3145728 | bytes 25165824 | tf_op jit(solution)/shard_map/concatenate | solution.py:49
  268.9 0.0 reduce-scatter.2.cloned.1.call-update
  268.9 212.2 %reduce-scatter.2.cloned.1.call-done = f32[256,3072]{1,0:T(8,128)} async-done(((f32[1024,3072]{1,0:T(8,128)}), f32[256,3072]{1,0:T(8,128)}) %reduce-scatter.2.cloned.1.call-update) | async-done | bytes 3145744 | tf_op jit(solution)/shard_map/reduce_scatter | solution.py:48
  481.1 2.4 copy.5
  483.5 5.3 %copy.6 = f32[256,6,1,512]{3,2,1,0:T(1,128)} copy(f32[256,6,1,512]{0,3,1,2:T(8,128)S(1)} %bitcast.16) | data formatting | bytes 6291456 | tf_op jit(solution)/shard_map/reshape | solution.py:55
  (3 shorter events, 0.0 us)
Async XLA Ops:
  6.5 148.5 %all-reduce.3.cloned.1.call-start = ((), (), s32[]{:S(2)}) async-start(), calls=%async_computation.2 | async-start | bytes 16777216 | tf_op jit(solution)/shard_map/psum | solution.py:9
  21.4 4.5 copy-start
  26.0 455.1 %reduce-scatter.2.cloned.1.call-start = ((), (), s32[]{:S(2)}) async-start(), calls=%async_computation.1 | async-start | bytes 15728640 | tf_op jit(solution)/shard_map/reduce_scatter | solution.py:48
  155.0 28.3 %slice-start = ((s8[20971520]{0:T(1024)(128)(4,1)}), s8[4194304]{0:T(1024)(128)(4,1)S(1)}, s32[]{:S(2)}) async-start(s8[20971520]{0:T(1024)(128)(4,1)} %bitcast.10), calls=%async_computation.3 | async-start | bytes 8388608
  155.0 28.3 %slice-start.1 = ((s8[20971520]{0:T(1024)(128)(4,1)}), s8[4194304]{0:T(1024)(128)(4,1)S(1)}, s32[]{:S(2)}) async-start(s8[20971520]{0:T(1024)(128)(4,1)} %bitcast.10), calls=%async_computation.4 | async-start | bytes 8388608
  160.0 5.2 %copy-start.1 = (f32[64,8,4,512]{3,1,2,0:T(8,128)S(1)}, f32[64,8,4,512]{3,1,2,0:T(8,128)}, u32[]{:S(2)}) copy-start(f32[64,8,4,512]{3,1,2,0:T(8,128)} %copy-done) | copy-start | bytes 12582916
  160.0 23.3 %slice-start.2 = ((s8[20971520]{0:T(1024)(128)(4,1)}), s8[4194304]{0:T(1024)(128)(4,1)S(1)}, s32[]{:S(2)}) async-start(s8[20971520]{0:T(1024)(128)(4,1)} %bitcast.10), calls=%async_computation.5 | async-start | bytes 8388608
  165.2 18.1 %slice-start.3 = ((s8[20971520]{0:T(1024)(128)(4,1)}), s8[4194304]{0:T(1024)(128)(4,1)S(1)}, s32[]{:S(2)}) async-start(s8[20971520]{0:T(1024)(128)(4,1)} %bitcast.10), calls=%async_computation.6 | async-start | bytes 8388608
  165.2 18.1 %slice-start.4 = ((s8[20971520]{0:T(1024)(128)(4,1)}), s8[4194304]{0:T(1024)(128)(4,1)S(1)}, s32[]{:S(2)}) async-start(s8[20971520]{0:T(1024)(128)(4,1)} %bitcast.10), calls=%async_computation.7 | async-start | bytes 8388608
Sparse Core Ops, SparseCore 0:
  26.1 128.9 all-reduce.2
  269.1 212.0 reduce-scatter.1
where the time goes:
time: 496 us
  waiting for transfers between devices  253 us (51%)
  local copies, waits for them, and re-layouts  121 us (24%)
  matrix products  93.5 us (19%)
  other arithmetic  14.5 us (3%)
  between operations  13.5 us (3%)
    reduce_scatter x1, waiting for transfers between devices, on_device(): lax.psum_scatter(jnp.concatenate([contract(panels, top_rows), ending], 1)...  212 us
    dot_general x2, matrix products, contract(): lax.dot_general(left, right, (((1,), (1,)), ((), ())), precision=lax.Prec...  93.5 us
    slice x1, local copies, waits for them, and re-layouts, on_device(): top_rows = blocks[:(row_blocks - 1) * block_size]  67.2 us
    psum x1, waiting for transfers between devices, broadcast(): return lax.psum(kept, axis)  40.6 us
    unnamed x17, local copies, waits for them, and re-layouts  28.2 us
    slice x1, local copies, waits for them, and re-layouts, on_device(): last_row = blocks[(row_blocks - 1) * block_size:]  12.9 us
    concatenate x1, other arithmetic, on_device(): jnp.concatenate([contract(panels, top_rows), ending], 1)  10.2 us
  transfers between devices with their start and end apart: 2, of which 2 were waited for; matrix products, arithmetic and copies ran while one was open for 18% of the time, Pallas kernels for 0%

commit v1 on v0

v1 whole, which is shorter than its diff:
```python
import functools

import jax
import jax.numpy as jnp
from jax import lax
from jax.experimental import pallas as pl
from jax.experimental.pallas import tpu as pltpu
from jax.sharding import PartitionSpec as P

LANES = 128
CHUNKS = 4
PREP_ROWS = 256


def split(value):
    high = value.astype(jnp.bfloat16)
    low = (value - high.astype(jnp.float32)).astype(jnp.bfloat16)
    return high, low


def prep_kernel(place, source, high_ref, low_ref, *, block_size, last_start, anchor, prow_size, pcol_size):
    rows, width = high_ref.shape
    groups = width // LANES
    start = pl.program_id(0) * rows

    def emit(masked):
        for group in range(groups):
            value = source[pl.ds(group, rows, stride=groups), :]
            if masked:
                col = group * LANES
                base = (col // block_size * pcol_size + place[1]) * block_size + col % block_size
                first = (last_start // block_size * prow_size + place[0]) * block_size
                row_ids = first + start - last_start + lax.broadcasted_iota(jnp.int32, value.shape, 0)
                col_ids = anchor + base + lax.broadcasted_iota(jnp.int32, value.shape, 1)
                value = jnp.where(row_ids <= col_ids, value, 0.0)
            high, low = split(value)
            at = pl.ds(group * LANES, LANES)
            high_ref[:, at] = high
            low_ref[:, at] = low

    @pl.when(start < last_start)
    def _():
        emit(False)

    @pl.when(start >= last_start)
    def _():
        emit(True)


def dot(left, right):
    return lax.dot_general(
        left, right, (((1,), (1,)), ((), ())), preferred_element_type=jnp.float32
    )


def product_kernel(first, second, high_ref, low_ref, out_ref, left_high, left_low):
    half = out_ref.shape[0] // 2
    groups = left_high.shape[1] // LANES

    @pl.when(pl.program_id(0) == 0)
    def _():
        for index, panel in enumerate((first, second)):
            for group in range(groups):
                high, low = split(panel[pl.ds(group, half, stride=groups), :])
                at = (pl.ds(index * half, half), pl.ds(group * LANES, LANES))
                left_high[at] = high
                left_low[at] = low

    out_ref[...] = (
        dot(left_high[...], low_ref[...])
        + dot(left_low[...], high_ref[...])
        + dot(left_high[...], high_ref[...])
    )


def tree_steps(count, upward):
    spans = []
    span = 1
    while span < count:
        spans.append(span)
        span *= 2
    have = [0]
    steps = []
    for span in spans if upward else spans[::-1]:
        sends = [(at, at + span) for at in have if at + span < count and at + span not in have]
        have += [to for _, to in sends]
        steps.append([(count - 1 - at, count - 1 - to) for at, to in sends])
    return steps


def broadcast(kept, prow_size, my_row):
    pairs = prow_size // 2
    held = kept
    for even, odd in zip(tree_steps(pairs, True), tree_steps(pairs, False)):
        moves = [(2 * a, 2 * b) for a, b in even] + [(2 * a + 1, 2 * b + 1) for a, b in odd]
        landed = lax.ppermute(held, "prow", moves)
        targets = jnp.array([any(to == row for _, to in moves) for row in range(prow_size)])
        held = jnp.where(targets[my_row], landed, held)
    other = lax.ppermute(held, "prow", [(row, row ^ 1) for row in range(prow_size)])
    is_even = my_row % 2 == 0
    return jnp.where(is_even, held, other), jnp.where(is_even, other, held)


def on_device(u_window):
    row_blocks = u_window.shape[0]
    block_size = u_window.shape[2]
    col_blocks = u_window.shape[3]
    prow_size = lax.axis_size("prow")
    pcol_size = lax.axis_size("pcol")
    my_row = lax.axis_index("prow")
    my_col = lax.axis_index("pcol")
    width = col_blocks * block_size
    groups = width // LANES
    rows = row_blocks * block_size
    last_start = rows - block_size
    anchor = (row_blocks * prow_size - 2) * block_size
    lines = u_window.reshape(rows * groups, LANES)

    last = lines[last_start * groups :].reshape(block_size, groups, LANES)
    row_ids = ((row_blocks - 1) * prow_size + my_row) * block_size + jnp.arange(
        block_size, dtype=jnp.int32
    )
    col_index = jnp.arange(width, dtype=jnp.int32)
    window_col = (
        col_index // block_size * pcol_size + my_col
    ) * block_size + col_index % block_size
    keep = row_ids[:, None, None] <= anchor + window_col.reshape(1, groups, LANES)
    masked = jnp.where(keep, last, 0.0)
    shares = pcol_size // 2
    part = block_size // shares // CHUNKS
    pieces = masked.reshape(shares, CHUNKS, part, groups, LANES)
    panels = [
        broadcast(pieces[:, k].reshape(shares * part * groups, LANES), prow_size, my_row)
        for k in range(CHUNKS)
    ]

    place = jnp.stack([my_row, my_col]).astype(jnp.int32)
    half = jax.ShapeDtypeStruct((rows, width), jnp.bfloat16)
    high, low = pl.pallas_call(
        functools.partial(
            prep_kernel,
            block_size=block_size,
            last_start=last_start,
            anchor=anchor,
            prow_size=prow_size,
            pcol_size=pcol_size,
        ),
        grid=(rows // PREP_ROWS,),
        in_specs=[
            pl.BlockSpec(memory_space=pltpu.SMEM),
            pl.BlockSpec((PREP_ROWS * groups, LANES), lambda i: (i, 0)),
        ],
        out_specs=[pl.BlockSpec((PREP_ROWS, width), lambda i: (i, 0))] * 2,
        out_shape=[half, half],
        cost_estimate=pl.CostEstimate(
            flops=10 * rows * width, bytes_accessed=8 * rows * width, transcendentals=0
        ),
        name="prep",
    )(place, lines)

    chunk_rows = 2 * shares * part
    multiply = pl.pallas_call(
        product_kernel,
        grid=(row_blocks,),
        in_specs=[pl.BlockSpec((shares * part * groups, LANES), lambda i: (0, 0))] * 2
        + [pl.BlockSpec((block_size, width), lambda i: (i, 0))] * 2,
        out_specs=pl.BlockSpec((chunk_rows, block_size), lambda i: (0, i)),
        out_shape=jax.ShapeDtypeStruct((chunk_rows, rows), jnp.float32),
        scratch_shapes=[pltpu.VMEM((chunk_rows, width), jnp.bfloat16)] * 2,
        cost_estimate=pl.CostEstimate(
            flops=6 * chunk_rows * rows * width,
            bytes_accessed=4 * rows * width + 4 * chunk_rows * rows,
            transcendentals=0,
        ),
        name="product",
    )
    summed = [
        lax.psum_scatter(
            multiply(first, second, high, low), "pcol", scatter_dimension=0, tiled=True
        )
        for first, second in panels
    ]
    share = jnp.concatenate(summed, 0)
    return share.reshape(share.shape[0], row_blocks, 1, block_size)


def solution(mesh):
    placed = (P(None, "prow", None, None, "pcol", None),)
    return jax.shard_map(
        on_device,
        mesh=mesh,
        in_specs=placed,
        out_specs=P("pcol", None, "prow", None),
        check_vma=False,
    )
```

time: 496 us -> 362 us (0.73)
  local copies, waits for them, and re-layouts: 121 us -> 16.7 us
  Pallas kernels: 0 us -> 94.2 us
  matrix products: 93.5 us -> 0 us
  waiting for transfers between devices: 253 us -> 211 us
  starting transfers between devices: 0.22 us -> 9.72 us
    reduce_scatter x1 -> x4, waiting for transfers between devices: 212 us -> 87.9 us  [on_device(): lax.psum_scatter(multiply(first, second, high, low), 'pcol', scatter_dime...]
    ppermute x0 -> x12, waiting for transfers between devices: none -> 123 us  [the longest x8 115 us: broadcast(): landed = lax.ppermute(held, 'prow', moves)]
    pallas_call x0 -> x5, Pallas kernels: none -> 94.2 us  [the longest x4 68 us: on_device(): multiply(first, second, high, low)]
    dot_general x2 -> x0, matrix products: 93.5 us -> none  [contract(): lax.dot_general(left, right, (((1,), (1,)), ((), ())), precision=lax.Prec...]
    slice x2 -> x3, local copies, waits for them, and re-layouts: 80.1 us -> 3.52 us  [the longest x2 2.18 us: on_device(): last = lines[last_start * groups:].reshape(block_size, groups, LANES)]
    psum x1 -> x0, waiting for transfers between devices: 40.6 us -> none  [broadcast(): return lax.psum(kept, axis)]
    unnamed x17 -> x6, local copies, waits for them, and re-layouts: 28.2 us -> 1.16 us
    ppermute x0 -> x12, starting transfers between devices: none -> 9.59 us  [the longest x8 9.3 us: broadcast(): landed = lax.ppermute(held, 'prow', moves)]
  transfers between devices with their start and end apart: 2 -> 16, of which waited for: 2 -> 9; matrix products, arithmetic and copies ran while one was open for 18% -> 3% of each run, Pallas kernels for 0% -> 21%
where the time goes in v1:
time: 362 us; the launch traced here: 361 us
  waiting for transfers between devices  211 us (58%)
  Pallas kernels  94.2 us (26%)
  local copies, waits for them, and re-layouts  16.7 us (5%)
  other arithmetic  16.3 us (5%)
  between operations  13.4 us (4%)
  starting transfers between devices  9.72 us (3%)
    ppermute x8, waiting for transfers between devices, broadcast(): landed = lax.ppermute(held, 'prow', moves)  115 us
    reduce_scatter x4, waiting for transfers between devices, on_device(): lax.psum_scatter(multiply(first, second, high, low), 'pcol', scatter_dime...  87.9 us
    pallas_call x4, Pallas kernels, on_device(): multiply(first, second, high, low)  68 us
    pallas_call x1, Pallas kernels, on_device(): pl.pallas_call(functools.partial(prep_kernel, block_size=block_size, last...  26.2 us
    ppermute x8, starting transfers between devices, broadcast(): landed = lax.ppermute(held, 'prow', moves)  9.3 us
    reshape x1, local copies, waits for them, and re-layouts, on_device(): return share.reshape(share.shape[0], row_blocks, 1, block_size)  8.45 us
    ppermute x4, waiting for transfers between devices, broadcast(): lax.ppermute(held, 'prow', [(row, row ^ 1) for row in range(prow_size)])  7.94 us
  transfers between devices with their start and end apart: 16, of which 9 were waited for; matrix products, arithmetic and copies ran while one was open for 3% of the time, Pallas kernels for 21%

profile of v1, /device:TPU:0, one launch (start us, length us, event | category | flops | bytes accessed | tf_op | source)
XLA Modules:
  0.0 361.5 jit_solution(15488459965775885501)
XLA Ops:
  6.6 0.0 slice-start
  6.6 2.2 slice-done
  8.8 0.6 copy_select_fusion
  9.4 0.0 copy-start.2
  9.4 1.3 fusion.10
  10.7 1.8 collective-permute-start
  12.5 0.6 dynamic_slice.25
  13.1 0.0 collective-permute-done
  13.1 0.8 broadcast_select_fusion.3
  13.9 1.3 collective-permute-start.1
  15.2 0.6 dynamic_slice.24
  15.8 30.8 %collective-permute-done.1 = f32[2048,128]{1,0:T(8,128)S(1)} collective-permute-done((f32[2048,128]{1,0:T(8,128)S(1)}, f32[2048,128]{1,0:T(8,128)S(1)}, u32[]{:S(2)}, u32[]{:S(2)}) %collective-permute-start.1) | collective-permute-done | bytes 1048608 | tf_op jit(solution)/shard_map/ppermute | solution.py:96
  46.6 0.7 broadcast_select_fusion.7
  47.3 0.1 collective-permute-start.2
  47.4 0.7 pad_add_fusion.place
  48.1 26.2 %prep.1 = (bf16[3072,2048]{1,0:T(8,128)(2,1)}, bf16[3072,2048]{1,0:T(8,128)(2,1)}) custom-call(s32[2]{0:T(128)} %pad_add_fusion.place, f32[49152,128]{1,0:T(8,128)} %bitcast.15), custom_call_target="tpu_custom_call" | custom-call | flops 62914560 | bytes 50331648 | tf_op jit(solution)/shard_map/prep/pallas_call | solution.py:139
  74.3 0.0 collective-permute-done.2
  74.3 2.8 broadcast_select_fusion.14
  77.1 17.1 %product.4 = f32[256,3072]{1,0:T(8,128)} custom-call(f32[2048,128]{1,0:T(8,128)} %get-tuple-element.14.first, f32[2048,128]{1,0:T(8,128)} %get-tuple-element.13.second, bf16[3072,2048]{1,0:T(8,128)(2,1)} %get-tuple-element.7.high_ref, bf16[3072,2048]{1,0:T(8,128)(2,1)} %get-tuple-element.8.low_ref), custom_call_target="tpu_custom_call" | custom-call | flops 9663676416 | bytes 28311552 | tf_op jit(solution)/shard_map/product/pallas_call | solution.py:179
  94.2 0.0 reduce-scatter.5.cloned.1.call-update
  94.2 0.0 reduce-scatter.7.cloned.1.call-start
  94.3 1.1 copy-done
  95.4 0.7 collective-permute-start.3
  96.1 0.0 collective-permute-done.3
  96.1 0.7 broadcast_select_fusion.2
  96.8 1.3 collective-permute-start.4
  98.1 28.2 %collective-permute-done.4 = f32[2048,128]{1,0:T(8,128)S(1)} collective-permute-done((f32[2048,128]{1,0:T(8,128)S(1)}, f32[2048,128]{1,0:T(8,128)S(1)}, u32[]{:S(2)}, u32[]{:S(2)}) %collective-permute-start.4) | collective-permute-done | bytes 1048608 | tf_op jit(solution)/shard_map/ppermute | solution.py:96
  126.4 0.7 broadcast_select_fusion.6
  127.1 0.1 collective-permute-start.5
  127.2 2.6 collective-permute-done.5
  129.8 1.5 broadcast_select_fusion.12
  131.3 16.9 %product.5 = f32[256,3072]{1,0:T(8,128)} custom-call(f32[2048,128]{1,0:T(8,128)} %get-tuple-element.16.first, f32[2048,128]{1,0:T(8,128)} %get-tuple-element.15.second, bf16[3072,2048]{1,0:T(8,128)(2,1)} %get-tuple-element.7.high_ref, bf16[3072,2048]{1,0:T(8,128)(2,1)} %get-tuple-element.8.low_ref), custom_call_target="tpu_custom_call" | custom-call | flops 9663676416 | bytes 28311552 | tf_op jit(solution)/shard_map/product/pallas_call | solution.py:179
  148.2 0.0 reduce-scatter.7.cloned.1.call-update
  148.2 0.0 reduce-scatter.9.cloned.1.call-start
  148.3 0.7 collective-permute-start.6
  149.0 0.0 collective-permute-done.6
  149.0 0.7 broadcast_select_fusion.1
  149.7 1.5 collective-permute-start.7
  151.2 28.1 %collective-permute-done.7 = f32[2048,128]{1,0:T(8,128)S(1)} collective-permute-done((f32[2048,128]{1,0:T(8,128)S(1)}, f32[2048,128]{1,0:T(8,128)S(1)}, u32[]{:S(2)}, u32[]{:S(2)}) %collective-permute-start.7) | collective-permute-done | bytes 1048608 | tf_op jit(solution)/shard_map/ppermute | solution.py:96
  179.3 0.7 broadcast_select_fusion.5
  180.1 0.1 collective-permute-start.8
  180.2 2.6 collective-permute-done.8
  182.8 1.4 broadcast_select_fusion.10
  184.3 17.1 %product.6 = f32[256,3072]{1,0:T(8,128)} custom-call(f32[2048,128]{1,0:T(8,128)} %get-tuple-element.18.first, f32[2048,128]{1,0:T(8,128)} %get-tuple-element.17.second, bf16[3072,2048]{1,0:T(8,128)(2,1)} %get-tuple-element.7.high_ref, bf16[3072,2048]{1,0:T(8,128)(2,1)} %get-tuple-element.8.low_ref), custom_call_target="tpu_custom_call" | custom-call | flops 9663676416 | bytes 28311552 | tf_op jit(solution)/shard_map/product/pallas_call | solution.py:179
  201.3 0.0 reduce-scatter.9.cloned.1.call-update
  201.4 0.0 reduce-scatter.11.cloned.1.call-start
  201.4 0.7 collective-permute-start.9
  202.2 0.0 collective-permute-done.9
  202.2 0.7 broadcast_select_fusion
  202.8 1.3 collective-permute-start.10
  204.1 28.1 %collective-permute-done.10 = f32[2048,128]{1,0:T(8,128)S(1)} collective-permute-done((f32[2048,128]{1,0:T(8,128)S(1)}, f32[2048,128]{1,0:T(8,128)S(1)}, u32[]{:S(2)}, u32[]{:S(2)}) %collective-permute-start.10) | collective-permute-done | bytes 1048608 | tf_op jit(solution)/shard_map/ppermute | solution.py:96
  232.3 0.7 broadcast_select_fusion.4
  233.0 0.1 collective-permute-start.11
  233.1 2.6 collective-permute-done.11
  235.8 1.5 broadcast_select_fusion.8
  237.2 16.9 %product.7 = f32[256,3072]{1,0:T(8,128)} custom-call(f32[2048,128]{1,0:T(8,128)} %get-tuple-element.20.first, f32[2048,128]{1,0:T(8,128)} %get-tuple-element.19.second, bf16[3072,2048]{1,0:T(8,128)(2,1)} %get-tuple-element.7.high_ref, bf16[3072,2048]{1,0:T(8,128)(2,1)} %get-tuple-element.8.low_ref), custom_call_target="tpu_custom_call" | custom-call | flops 9663676416 | bytes 28311552 | tf_op jit(solution)/shard_map/product/pallas_call | solution.py:179
  254.1 0.0 reduce-scatter.11.cloned.1.call-update
  254.1 0.0 reduce-scatter.5.cloned.1.call-done
  254.2 0.0 reduce-scatter.7.cloned.1.call-done
  254.2 25.4 %reduce-scatter.9.cloned.1.call-done = f32[64,3072]{1,0:T(8,128)} async-done(((f32[256,3072]{1,0:T(8,128)}), f32[64,3072]{1,0:T(8,128)}) %reduce-scatter.9.cloned.1.call-update) | async-done | bytes 786448 | tf_op jit(solution)/shard_map/reduce_scatter | solution.py:178
  279.6 62.5 %reduce-scatter.11.cloned.1.call-done = f32[64,3072]{1,0:T(8,128)} async-done(((f32[256,3072]{1,0:T(8,128)}), f32[64,3072]{1,0:T(8,128)}) %reduce-scatter.11.cloned.1.call-update) | async-done | bytes 786448 | tf_op jit(solution)/shard_map/reduce_scatter | solution.py:178
  342.1 2.1 pad_maximum_fusion
  344.1 2.3 copy.13
  346.5 8.4 %copy.14 = f32[256,6,1,512]{3,2,1,0:T(1,128)} copy(f32[256,6,1,512]{0,3,1,2:T(8,128)} %bitcast.17) | data formatting | bytes 6291456 | tf_op jit(solution)/shard_map/reshape | solution.py:184
  (7 shorter events, 0.0 us)
Async XLA Ops:
  6.5 247.6 %reduce-scatter.5.cloned.1.call-start = ((), (), s32[]{:S(2)}) async-start(), calls=%async_computation.4 | async-start | bytes 3932160 | tf_op jit(solution)/shard_map/reduce_scatter | solution.py:178
  6.6 2.2 slice-start
  9.4 3.1 copy-start.2
  10.7 4.5 %copy-start.1 = (pred[8]{0:T(512)(128)(4,1)S(1)}, pred[8]{0:T(512)(128)(4,1)}, u32[]{:S(2)}) copy-start(pred[8]{0:T(512)(128)(4,1)} %constant.84.clone) | copy-start | bytes 28
  10.7 2.4 collective-permute-start
  13.9 32.7 %collective-permute-start.1 = (f32[2048,128]{1,0:T(8,128)S(1)}, f32[2048,128]{1,0:T(8,128)S(1)}, u32[]{:S(2)}, u32[]{:S(2)}) collective-permute-start(f32[2048,128]{1,0:T(8,128)S(1)} %broadcast_select_fusion.3), channel_id=1, source_target_pairs={{24,8},{16,0},{28,20},{12,4},{25,9},{17,1},{29,21},{13,5},{26,10},... | collective-permute-start | bytes 3145736 | tf_op jit(solution)/shard_map/ppermute | solution.py:96
  47.3 27.0 %collective-permute-start.2 = (f32[2048,128]{1,0:T(8,128)S(1)}, f32[2048,128]{1,0:T(8,128)}, u32[]{:S(2)}, u32[]{:S(2)}) collective-permute-start(f32[2048,128]{1,0:T(8,128)S(1)} %broadcast_select_fusion.7), channel_id=1, source_target_pairs={{0,4},{4,0},{8,12},{12,8},{16,20},{20,16},{24,28},{28,24},{1,5},{5... | collective-permute-start | bytes 3145736 | tf_op jit(solution)/shard_map/ppermute | solution.py:99
  94.2 1.2 copy-start
  94.2 160.0 %reduce-scatter.7.cloned.1.call-start = ((), (), s32[]{:S(2)}) async-start(), calls=%async_computation.5 | async-start | bytes 3932160 | tf_op jit(solution)/shard_map/reduce_scatter | solution.py:178
  95.4 0.7 collective-permute-start.3
  96.8 29.5 %collective-permute-start.4 = (f32[2048,128]{1,0:T(8,128)S(1)}, f32[2048,128]{1,0:T(8,128)S(1)}, u32[]{:S(2)}, u32[]{:S(2)}) collective-permute-start(f32[2048,128]{1,0:T(8,128)S(1)} %broadcast_select_fusion.2), channel_id=1, source_target_pairs={{24,8},{16,0},{28,20},{12,4},{25,9},{17,1},{29,21},{13,5},{26,10},... | collective-permute-start | bytes 3145736 | tf_op jit(solution)/shard_map/ppermute | solution.py:96
  127.1 2.7 collective-permute-start.5
  148.2 131.3 %reduce-scatter.9.cloned.1.call-start = ((), (), s32[]{:S(2)}) async-start(), calls=%async_computation.6 | async-start | bytes 3932160 | tf_op jit(solution)/shard_map/reduce_scatter | solution.py:178
  148.3 0.7 collective-permute-start.6
  149.7 29.6 %collective-permute-start.7 = (f32[2048,128]{1,0:T(8,128)S(1)}, f32[2048,128]{1,0:T(8,128)S(1)}, u32[]{:S(2)}, u32[]{:S(2)}) collective-permute-start(f32[2048,128]{1,0:T(8,128)S(1)} %broadcast_select_fusion.1), channel_id=1, source_target_pairs={{24,8},{16,0},{28,20},{12,4},{25,9},{17,1},{29,21},{13,5},{26,10},... | collective-permute-start | bytes 3145736 | tf_op jit(solution)/shard_map/ppermute | solution.py:96
  180.1 2.7 collective-permute-start.8
  201.4 140.7 %reduce-scatter.11.cloned.1.call-start = ((), (), s32[]{:S(2)}) async-start(), calls=%async_computation.7 | async-start | bytes 3932160 | tf_op jit(solution)/shard_map/reduce_scatter | solution.py:178
  201.4 0.7 collective-permute-start.9
  202.8 29.4 %collective-permute-start.10 = (f32[2048,128]{1,0:T(8,128)S(1)}, f32[2048,128]{1,0:T(8,128)S(1)}, u32[]{:S(2)}, u32[]{:S(2)}) collective-permute-start(f32[2048,128]{1,0:T(8,128)S(1)} %broadcast_select_fusion), channel_id=1, source_target_pairs={{24,8},{16,0},{28,20},{12,4},{25,9},{17,1},{29,21},{13,5},{26,10},... | collective-permute-start | bytes 3145736 | tf_op jit(solution)/shard_map/ppermute | solution.py:96
  233.0 2.7 collective-permute-start.11
Sparse Core Ops, SparseCore 0:
  94.3 59.8 reduce-scatter.4
  156.5 60.2 reduce-scatter.6
  219.2 60.3 reduce-scatter.8
  281.7 60.3 reduce-scatter.10

commit v2 on v1

--- a/solution.py
+++ b/solution.py
@@ -7,8 +7,9 @@
 from jax.experimental.pallas import tpu as pltpu
 from jax.sharding import PartitionSpec as P
 
+
 LANES = 128
-CHUNKS = 4
+SIXTEENTHS = (3, 5, 8)
 PREP_ROWS = 256
 
 
@@ -18,10 +19,13 @@
     return high, low
 
 
-def prep_kernel(place, source, high_ref, low_ref, *, block_size, last_start, anchor, prow_size, pcol_size):
+def prep_kernel(
+    place, source, *refs, begin, block_size, last_start, anchor, prow_size, pcol_size
+):
+    high_ref, low_ref = refs[-2:]
     rows, width = high_ref.shape
     groups = width // LANES
-    start = pl.program_id(0) * rows
+    start = begin + pl.program_id(0) * rows
 
     def emit(masked):
         for group in range(groups):
@@ -54,8 +58,11 @@
 
 
 def product_kernel(first, second, high_ref, low_ref, out_ref, left_high, left_low):
-    half = out_ref.shape[0] // 2
+    half = left_high.shape[0] // 2
     groups = left_high.shape[1] // LANES
+    block_size = high_ref.shape[0]
+    lines = out_ref.shape[0] // left_high.shape[0]
+    step = pl.program_id(0)
 
     @pl.when(pl.program_id(0) == 0)
     def _():
@@ -66,11 +73,16 @@
                 left_high[at] = high
                 left_low[at] = low
 
-    out_ref[...] = (
+    result = (
         dot(left_high[...], low_ref[...])
         + dot(left_low[...], high_ref[...])
         + dot(left_high[...], high_ref[...])
     )
+    spans = block_size // LANES
+    for span in range(spans):
+        out_ref[pl.ds(step * spans + span, 2 * half, stride=lines), :] = result[
+            :, span * LANES : (span + 1) * LANES
+        ]
 
 
 def tree_steps(count, upward):
@@ -91,11 +103,12 @@
 def broadcast(kept, prow_size, my_row):
     pairs = prow_size // 2
     held = kept
-    for even, odd in zip(tree_steps(pairs, True), tree_steps(pairs, False)):
+    steps = zip(tree_steps(pairs, True), tree_steps(pairs, False))
+    for even, odd in steps:
         moves = [(2 * a, 2 * b) for a, b in even] + [(2 * a + 1, 2 * b + 1) for a, b in odd]
         landed = lax.ppermute(held, "prow", moves)
-        targets = jnp.array([any(to == row for _, to in moves) for row in range(prow_size)])
-        held = jnp.where(targets[my_row], landed, held)
+        is_target = functools.reduce(jnp.logical_or, [my_row == to for _, to in moves])
+        held = jnp.where(is_target, landed, held)
     other = lax.ppermute(held, "prow", [(row, row ^ 1) for row in range(prow_size)])
     is_even = my_row % 2 == 0
     return jnp.where(is_even, held, other), jnp.where(is_even, other, held)
@@ -127,61 +140,67 @@
     keep = row_ids[:, None, None] <= anchor + window_col.reshape(1, groups, LANES)
     masked = jnp.where(keep, last, 0.0)
     shares = pcol_size // 2
-    part = block_size // shares // CHUNKS
-    pieces = masked.reshape(shares, CHUNKS, part, groups, LANES)
-    panels = [
-        broadcast(pieces[:, k].reshape(shares * part * groups, LANES), prow_size, my_row)
-        for k in range(CHUNKS)
-    ]
+    share_rows = block_size // shares
+    shaped = masked.reshape(shares, share_rows, groups, LANES)
+    parts = [count * share_rows // sum(SIXTEENTHS) for count in SIXTEENTHS]
+    panels = []
+    at = 0
+    for part in parts:
+        piece = shaped[:, at : at + part].reshape(shares * part * groups, LANES)
+        panels.append(broadcast(piece, prow_size, my_row))
+        at += part
 
     place = jnp.stack([my_row, my_col]).astype(jnp.int32)
-    half = jax.ShapeDtypeStruct((rows, width), jnp.bfloat16)
-    high, low = pl.pallas_call(
-        functools.partial(
-            prep_kernel,
-            block_size=block_size,
-            last_start=last_start,
-            anchor=anchor,
-            prow_size=prow_size,
-            pcol_size=pcol_size,
-        ),
-        grid=(rows // PREP_ROWS,),
-        in_specs=[
-            pl.BlockSpec(memory_space=pltpu.SMEM),
-            pl.BlockSpec((PREP_ROWS * groups, LANES), lambda i: (i, 0)),
-        ],
-        out_specs=[pl.BlockSpec((PREP_ROWS, width), lambda i: (i, 0))] * 2,
-        out_shape=[half, half],
-        cost_estimate=pl.CostEstimate(
-            flops=10 * rows * width, bytes_accessed=8 * rows * width, transcendentals=0
-        ),
-        name="prep",
-    )(place, lines)
-
-    chunk_rows = 2 * shares * part
-    multiply = pl.pallas_call(
-        product_kernel,
-        grid=(row_blocks,),
-        in_specs=[pl.BlockSpec((shares * part * groups, LANES), lambda i: (0, 0))] * 2
-        + [pl.BlockSpec((block_size, width), lambda i: (i, 0))] * 2,
-        out_specs=pl.BlockSpec((chunk_rows, block_size), lambda i: (0, i)),
-        out_shape=jax.ShapeDtypeStruct((chunk_rows, rows), jnp.float32),
-        scratch_shapes=[pltpu.VMEM((chunk_rows, width), jnp.bfloat16)] * 2,
-        cost_estimate=pl.CostEstimate(
-            flops=6 * chunk_rows * rows * width,
-            bytes_accessed=4 * rows * width + 4 * chunk_rows * rows,
-            transcendentals=0,
-        ),
-        name="product",
-    )
-    summed = [
-        lax.psum_scatter(
-            multiply(first, second, high, low), "pcol", scatter_dimension=0, tiled=True
-        )
-        for first, second in panels
-    ]
-    share = jnp.concatenate(summed, 0)
-    return share.reshape(share.shape[0], row_blocks, 1, block_size)
+    halves = ()
+    steps = rows // PREP_ROWS // 2
+    for index in range(2):
+        first_step = index * steps
+        halves = pl.pallas_call(
+            functools.partial(
+                prep_kernel,
+                begin=first_step * PREP_ROWS,
+                block_size=block_size,
+                last_start=last_start,
+                anchor=anchor,
+                prow_size=prow_size,
+                pcol_size=pcol_size,
+            ),
+            grid=(steps,),
+            in_specs=[
+                pl.BlockSpec(memory_space=pltpu.SMEM),
+                pl.BlockSpec((PREP_ROWS * groups, LANES), lambda i, base=first_step: (base + i, 0)),
+            ]
+            + [pl.BlockSpec(memory_space=pl.ANY)] * len(halves),
+            out_specs=[pl.BlockSpec((PREP_ROWS, width), lambda i, base=first_step: (base + i, 0))]
+            * 2,
+            out_shape=[jax.ShapeDtypeStruct((rows, width), jnp.bfloat16)] * 2,
+            input_output_aliases={2: 0, 3: 1} if halves else {},
+            cost_estimate=pl.CostEstimate(
+                flops=10 * rows * width, bytes_accessed=4 * rows * width, transcendentals=0
+            ),
+        )(place, lines, *halves)
+    high, low = halves
+
+    summed = []
+    lines_out = rows // LANES
+    for part, (first, second) in zip(parts, panels):
+        chunk_rows = 2 * shares * part
+        partial = pl.pallas_call(
+            product_kernel,
+            grid=(row_blocks,),
+            in_specs=[pl.BlockSpec((shares * part * groups, LANES), lambda i: (0, 0))] * 2
+            + [pl.BlockSpec((block_size, width), lambda i: (i, 0))] * 2,
+            out_specs=pl.BlockSpec((chunk_rows * lines_out, LANES), lambda i: (0, 0)),
+            out_shape=jax.ShapeDtypeStruct((chunk_rows * lines_out, LANES), jnp.float32),
+            scratch_shapes=[pltpu.VMEM((chunk_rows, width), jnp.bfloat16)] * 2,
+            cost_estimate=pl.CostEstimate(
+                flops=6 * chunk_rows * rows * width,
+                bytes_accessed=4 * rows * width + 4 * chunk_rows * rows,
+                transcendentals=0,
+            ),
+        )(first, second, high, low)
+        summed.append(lax.psum_scatter(partial, "pcol", scatter_dimension=0, tiled=True))
+    return jnp.concatenate(summed, 0).reshape(2 * block_size // pcol_size, row_blocks, 1, block_size)
 
 
 def solution(mesh):

time: 362 us -> 337 us (0.931)
  waiting for transfers between devices: 211 us -> 196 us
  local copies, waits for them, and re-layouts: 16.7 us -> 5.73 us
    ppermute x8 -> x6, waiting for transfers between devices: 115 us -> 20.7 us  [broadcast(): landed = lax.ppermute(held, 'prow', moves)]
    reduce_scatter x4 -> x3, waiting for transfers between devices: 87.9 us -> 170 us  [on_device(): lax.psum_scatter(partial, 'pcol', scatter_dimension=0, tiled=True)]
    reshape x1 -> x0, local copies, waits for them, and re-layouts: 8.45 us -> none  [on_device(): return share.reshape(share.shape[0], row_blocks, 1, block_size)]
    ppermute x4 -> x3, waiting for transfers between devices: 7.94 us -> 4.84 us  [broadcast(): lax.ppermute(held, 'prow', [(row, row ^ 1) for row in range(prow_size)])]
    ppermute x8 -> x6, starting transfers between devices: 9.3 us -> 8.7 us  [broadcast(): landed = lax.ppermute(held, 'prow', moves)]
  transfers between devices with their start and end apart: 16 -> 12, of which waited for: 9 -> 6; matrix products, arithmetic and copies ran while one was open for 3% -> 4% of each run, Pallas kernels for 21% -> 28%
where the time goes in v2:
time: 337 us; the launch traced here: 336 us
  waiting for transfers between devices  196 us (58%)
  Pallas kernels  94.2 us (28%)
  other arithmetic  16.3 us (5%)
  between operations  13.3 us (4%)
  starting transfers between devices  10.8 us (3%)
  local copies, waits for them, and re-layouts  5.73 us (2%)
    reduce_scatter x3, waiting for transfers between devices, on_device(): lax.psum_scatter(partial, 'pcol', scatter_dimension=0, tiled=True)  170 us
    pallas_call x3, Pallas kernels, on_device(): pl.pallas_call(product_kernel, grid=(row_blocks,), in_specs=[pl.BlockSpec...  67.2 us
    pallas_call x2, Pallas kernels, on_device(): pl.pallas_call(functools.partial(prep_kernel, begin=first_step * PREP_ROW...  27 us
    ppermute x6, waiting for transfers between devices, broadcast(): landed = lax.ppermute(held, 'prow', moves)  20.7 us
    ppermute x6, starting transfers between devices, broadcast(): landed = lax.ppermute(held, 'prow', moves)  8.7 us
  transfers between devices with their start and end apart: 12, of which 6 were waited for; matrix products, arithmetic and copies ran while one was open for 4% of the time, Pallas kernels for 28%

profile of v2, /device:TPU:0, one launch (start us, length us, event | category | flops | bytes accessed | tf_op | source)
XLA Modules:
  0.0 336.0 jit_solution(10465858313531814517)
XLA Ops:
  6.5 0.0 reduce-scatter.4.cloned.1.call-start
  6.6 0.0 slice-start
  6.6 2.2 slice-done
  8.8 0.7 compare_select_fusion
  9.5 0.0 copy-start
  9.5 1.9 copy-done
  11.4 0.1 slice.17
  11.5 0.7 collective-permute-start
  12.2 0.0 copy-start.1
  12.2 0.0 collective-permute-done
  12.2 1.0 broadcast_select_fusion.8
  13.2 1.4 collective-permute-start.1
  14.6 1.4 slice.18
  16.0 1.8 collective-permute-start.3
  17.8 0.0 copy-done.1
  17.8 0.1 slice.19
  17.9 0.0 copy-start.2
  17.9 2.1 collective-permute-start.6
  20.0 0.6 pad_add_fusion.place
  20.6 13.2 %shard_map.17 = (bf16[3072,2048]{1,0:T(8,128)(2,1)}, bf16[3072,2048]{1,0:T(8,128)(2,1)}) custom-call(s32[2]{0:T(128)} %pad_add_fusion.place, f32[49152,128]{1,0:T(8,128)} %bitcast.11), custom_call_target="tpu_custom_call" | custom-call | flops 62914560 | bytes 25165824 | tf_op jit(solution)/shard_map/pallas_call | solution.py:158
  33.8 0.0 copy-done.2
  33.8 13.8 %shard_map.18 = (bf16[3072,2048]{1,0:T(8,128)(2,1)}, bf16[3072,2048]{1,0:T(8,128)(2,1)}) custom-call(s32[2]{0:T(128)} %pad_add_fusion.place, f32[49152,128]{1,0:T(8,128)} %bitcast.12, bf16[3072,2048]{1,0:T(8,128)(2,1)} %get-tuple-element.9.refs_0_, bf16[3072,2048]{1,0:T(8,128)(2,1)} %get-tuple-element.10.refs_1_), custom_call_target="tpu_custom_call", output_to_operand_aliasing={{0}: (2, {}), {1}: (3, {})} | custom-call | flops 62914560 | bytes 25165824 | tf_op jit(solution)/shard_map/pallas_call | solution.py:158
  47.6 0.0 collective-permute-done.1
  47.6 1.2 broadcast_select_fusion.9
  48.9 0.6 collective-permute-start.2
  49.4 0.0 collective-permute-done.3
  49.4 1.4 broadcast_select_fusion.4
  50.8 1.3 collective-permute-start.4
  52.1 0.0 collective-permute-done.2
  52.1 1.3 broadcast_select_fusion.10
  53.4 17.8 %shard_map.19 = f32[4608,128]{1,0:T(8,128)} custom-call(f32[1536,128]{1,0:T(8,128)} %get-tuple-element.18.first, f32[1536,128]{1,0:T(8,128)} %get-tuple-element.17.second, bf16[3072,2048]{1,0:T(8,128)(2,1)} %get-tuple-element.11.high_ref, bf16[3072,2048]{1,0:T(8,128)(2,1)} %get-tuple-element.12.low_ref), custom_call_target="tpu_custom_call" | custom-call | flops 7247757312 | bytes 27525120 | tf_op jit(solution)/shard_map/pallas_call | solution.py:188
  71.2 0.0 reduce-scatter.4.cloned.1.call-update
  71.2 0.0 reduce-scatter.6.cloned.1.call-start
  71.3 0.0 copy-start.3
  71.3 13.0 %collective-permute-done.4 = f32[2560,128]{1,0:T(8,128)S(1)} collective-permute-done((f32[2560,128]{1,0:T(8,128)}, f32[2560,128]{1,0:T(8,128)S(1)}, u32[]{:S(2)}, u32[]{:S(2)}) %collective-permute-start.4) | collective-permute-done | bytes 1310752 | tf_op jit(solution)/shard_map/ppermute | solution.py:109
  84.3 0.1 broadcast_select_fusion.5
  84.4 0.1 collective-permute-start.5
  84.5 0.0 collective-permute-done.6
  84.5 0.0 copy-done.3
  84.5 0.5 broadcast_select_fusion
  85.0 1.5 collective-permute-start.7
  86.4 1.1 collective-permute-done.5
  87.5 1.7 broadcast_select_fusion.6
  89.2 20.0 %shard_map.20 = f32[7680,128]{1,0:T(8,128)} custom-call(f32[2560,128]{1,0:T(8,128)} %get-tuple-element.16.first, f32[2560,128]{1,0:T(8,128)} %get-tuple-element.15.second, bf16[3072,2048]{1,0:T(8,128)(2,1)} %get-tuple-element.11.high_ref, bf16[3072,2048]{1,0:T(8,128)(2,1)} %get-tuple-element.12.low_ref), custom_call_target="tpu_custom_call" | custom-call | flops 12079595520 | bytes 29097984 | tf_op jit(solution)/shard_map/pallas_call | solution.py:188
  109.2 0.0 reduce-scatter.6.cloned.1.call-update
  109.2 0.0 reduce-scatter.8.cloned.1.call-start
  109.3 7.7 %collective-permute-done.7 = f32[4096,128]{1,0:T(8,128)} collective-permute-done((f32[4096,128]{1,0:T(8,128)S(1)}, f32[4096,128]{1,0:T(8,128)}, u32[]{:S(2)}, u32[]{:S(2)}) %collective-permute-start.7) | collective-permute-done | bytes 2097184 | tf_op jit(solution)/shard_map/ppermute | solution.py:109
  117.0 1.8 broadcast_select_fusion.1
  118.8 1.3 collective-permute-start.8
  120.1 3.8 %collective-permute-done.8 = f32[4096,128]{1,0:T(8,128)S(1)} collective-permute-done((f32[4096,128]{1,0:T(8,128)S(1)}, f32[4096,128]{1,0:T(8,128)S(1)}, u32[]{:S(2)}, u32[]{:S(2)}) %collective-permute-start.8) | collective-permute-done | bytes 2097184 | tf_op jit(solution)/shard_map/ppermute | solution.py:112
  123.9 2.2 broadcast_select_fusion.2
  126.1 29.4 %shard_map.21 = f32[12288,128]{1,0:T(8,128)} custom-call(f32[4096,128]{1,0:T(8,128)} %get-tuple-element.14.first, f32[4096,128]{1,0:T(8,128)} %get-tuple-element.13.second, bf16[3072,2048]{1,0:T(8,128)(2,1)} %get-tuple-element.11.high_ref, bf16[3072,2048]{1,0:T(8,128)(2,1)} %get-tuple-element.12.low_ref), custom_call_target="tpu_custom_call" | custom-call | flops 19327352832 | bytes 31457280 | tf_op jit(solution)/shard_map/pallas_call | solution.py:188
  155.5 0.0 reduce-scatter.8.cloned.1.call-update
  155.5 0.0 reduce-scatter.4.cloned.1.call-done
  155.5 56.7 %reduce-scatter.6.cloned.1.call-done = f32[1920,128]{1,0:T(8,128)} async-done(((f32[7680,128]{1,0:T(8,128)}), f32[1920,128]{1,0:T(8,128)}) %reduce-scatter.6.cloned.1.call-update) | async-done | bytes 983056 | tf_op jit(solution)/shard_map/reduce_scatter | solution.py:202
  212.2 113.6 %reduce-scatter.8.cloned.1.call-done = f32[3072,128]{1,0:T(8,128)} async-done(((f32[12288,128]{1,0:T(8,128)}), f32[3072,128]{1,0:T(8,128)}) %reduce-scatter.8.cloned.1.call-update) | async-done | bytes 1572880 | tf_op jit(solution)/shard_map/reduce_scatter | solution.py:202
  325.8 3.7 %pad_maximum_fusion = f32[6144,128]{1,0:T(8,128)} fusion(f32[3072,128]{1,0:T(8,128)} %reduce-scatter.8.cloned.1.call-done, f32[1920,128]{1,0:T(8,128)} %reduce-scatter.6.cloned.1.call-done, f32[1152,128]{1,0:T(8,128)} %reduce-scatter.4.cloned.1.call-done), kind=kLoop, calls=%fused_computation.1 | loop fusion | flops 1572864 | bytes 6291456 | tf_op jit(solution)/shard_map/concatenate | solution.py:203
  (2 shorter events, 0.0 us)
Async XLA Ops:
  6.5 149.0 %reduce-scatter.4.cloned.1.call-start = ((), (), s32[]{:S(2)}) async-start(), calls=%async_computation.3 | async-start | bytes 2949120 | tf_op jit(solution)/shard_map/reduce_scatter | solution.py:202
  6.6 2.2 slice-start
  9.5 1.9 copy-start
  11.5 0.7 collective-permute-start
  12.2 5.6 %copy-start.1 = (f32[2,256,16,128]{3,2,1,0:T(8,128)S(1)}, f32[2,256,16,128]{3,2,1,0:T(8,128)}, u32[]{:S(2)}) copy-start(f32[2,256,16,128]{3,2,1,0:T(8,128)} %copy-done) | copy-start | bytes 12582916
  13.2 34.5 %collective-permute-start.1 = (f32[1536,128]{1,0:T(8,128)}, f32[1536,128]{1,0:T(8,128)}, u32[]{:S(2)}, u32[]{:S(2)}) collective-permute-start(f32[1536,128]{1,0:T(8,128)} %broadcast_select_fusion.8), channel_id=1, source_target_pairs={{24,8},{16,0},{28,20},{12,4},{25,9},{17,1},{29,21},{13,5},{26,10},... | collective-permute-start | bytes 2359304 | tf_op jit(solution)/shard_map/ppermute | solution.py:109
  16.0 33.4 %collective-permute-start.3 = (f32[2560,128]{1,0:T(8,128)S(1)}, f32[2560,128]{1,0:T(8,128)}, u32[]{:S(2)}, u32[]{:S(2)}) collective-permute-start(f32[2560,128]{1,0:T(8,128)S(1)} %bitcast.15), channel_id=1, source_target_pairs={{24,16},{28,12},{25,17},{29,13},{26,18},{30,14},{27,19},{31,15}} | collective-permute-start | bytes 3932168 | tf_op jit(solution)/shard_map/ppermute | solution.py:109
  17.9 15.9 %copy-start.2 = (f32[2,128,16,128]{3,2,1,0:T(8,128)}, f32[2,128,16,128]{3,2,1,0:T(8,128)S(1)}, u32[]{:S(2)}) copy-start(f32[2,128,16,128]{3,2,1,0:T(8,128)S(1)} %slice.19) | copy-start | bytes 6291460
  17.9 66.5 %collective-permute-start.6 = (f32[4096,128]{1,0:T(8,128)S(1)}, f32[4096,128]{1,0:T(8,128)}, u32[]{:S(2)}, u32[]{:S(2)}) collective-permute-start(f32[4096,128]{1,0:T(8,128)S(1)} %bitcast.14), channel_id=1, source_target_pairs={{24,16},{28,12},{25,17},{29,13},{26,18},{30,14},{27,19},{31,15}} | collective-permute-start | bytes 6291464 | tf_op jit(solution)/shard_map/ppermute | solution.py:109
  48.9 3.2 collective-permute-start.2
  50.8 33.5 %collective-permute-start.4 = (f32[2560,128]{1,0:T(8,128)}, f32[2560,128]{1,0:T(8,128)S(1)}, u32[]{:S(2)}, u32[]{:S(2)}) collective-permute-start(f32[2560,128]{1,0:T(8,128)} %broadcast_select_fusion.4), channel_id=1, source_target_pairs={{24,8},{16,0},{28,20},{12,4},{25,9},{17,1},{29,21},{13,5},{26,10},... | collective-permute-start | bytes 3932168 | tf_op jit(solution)/shard_map/ppermute | solution.py:109
  71.2 141.0 %reduce-scatter.6.cloned.1.call-start = ((), (), s32[]{:S(2)}) async-start(), calls=%async_computation.4 | async-start | bytes 4915200 | tf_op jit(solution)/shard_map/reduce_scatter | solution.py:202
  71.3 13.2 %copy-start.3 = (f32[2,128,16,128]{3,2,1,0:T(8,128)S(1)}, f32[2,128,16,128]{3,2,1,0:T(8,128)}, u32[]{:S(2)}) copy-start(f32[2,128,16,128]{3,2,1,0:T(8,128)} %copy-done.2) | copy-start | bytes 6291460
  84.4 3.1 collective-permute-start.5
  85.0 32.0 %collective-permute-start.7 = (f32[4096,128]{1,0:T(8,128)S(1)}, f32[4096,128]{1,0:T(8,128)}, u32[]{:S(2)}, u32[]{:S(2)}) collective-permute-start(f32[4096,128]{1,0:T(8,128)S(1)} %broadcast_select_fusion), channel_id=1, source_target_pairs={{24,8},{16,0},{28,20},{12,4},{25,9},{17,1},{29,21},{13,5},{26,10},... | collective-permute-start | bytes 6291464 | tf_op jit(solution)/shard_map/ppermute | solution.py:109
  109.2 216.5 %reduce-scatter.8.cloned.1.call-start = ((), (), s32[]{:S(2)}) async-start(), calls=%async_computation.5 | async-start | bytes 7864320 | tf_op jit(solution)/shard_map/reduce_scatter | solution.py:202
  118.8 5.1 %collective-permute-start.8 = (f32[4096,128]{1,0:T(8,128)S(1)}, f32[4096,128]{1,0:T(8,128)S(1)}, u32[]{:S(2)}, u32[]{:S(2)}) collective-permute-start(f32[4096,128]{1,0:T(8,128)S(1)} %broadcast_select_fusion.1), channel_id=1, source_target_pairs={{0,4},{4,0},{8,12},{12,8},{16,20},{20,16},{24,28},{28,24},{1,5},{5... | collective-permute-start | bytes 6291464 | tf_op jit(solution)/shard_map/ppermute | solution.py:112
Sparse Core Ops, SparseCore 0:
  71.3 66.5 reduce-scatter.3
  140.2 71.9 reduce-scatter.5
  214.5 111.2 reduce-scatter.7

commit v3 on v2

--- a/solution.py
+++ b/solution.py
@@ -57,11 +57,11 @@
     )
 
 
-def product_kernel(first, second, high_ref, low_ref, out_ref, left_high, left_low):
-    half = left_high.shape[0] // 2
-    groups = left_high.shape[1] // LANES
+def product_kernel(first, second, high_ref, low_ref, out_ref, left):
+    half = left.shape[0] // 4
+    groups = left.shape[1] // LANES
     block_size = high_ref.shape[0]
-    lines = out_ref.shape[0] // left_high.shape[0]
+    lines = out_ref.shape[0] // (2 * half)
     step = pl.program_id(0)
 
     @pl.when(pl.program_id(0) == 0)
@@ -69,15 +69,13 @@
         for index, panel in enumerate((first, second)):
             for group in range(groups):
                 high, low = split(panel[pl.ds(group, half, stride=groups), :])
-                at = (pl.ds(index * half, half), pl.ds(group * LANES, LANES))
-                left_high[at] = high
-                left_low[at] = low
-
-    result = (
-        dot(left_high[...], low_ref[...])
-        + dot(left_low[...], high_ref[...])
-        + dot(left_high[...], high_ref[...])
-    )
+                at = pl.ds(group * LANES, LANES)
+                left[pl.ds(index * half, half), at] = high
+                left[pl.ds((2 + index) * half, half), at] = low
+
+    by_high = dot(left[...], high_ref[...])
+    by_low = dot(left[: 2 * half], low_ref[...])
+    result = by_low + by_high[2 * half :] + by_high[: 2 * half]
     spans = block_size // LANES
     for span in range(spans):
         out_ref[pl.ds(step * spans + span, 2 * half, stride=lines), :] = result[
@@ -192,7 +190,7 @@
             + [pl.BlockSpec((block_size, width), lambda i: (i, 0))] * 2,
             out_specs=pl.BlockSpec((chunk_rows * lines_out, LANES), lambda i: (0, 0)),
             out_shape=jax.ShapeDtypeStruct((chunk_rows * lines_out, LANES), jnp.float32),
-            scratch_shapes=[pltpu.VMEM((chunk_rows, width), jnp.bfloat16)] * 2,
+            scratch_shapes=[pltpu.VMEM((2 * chunk_rows, width), jnp.bfloat16)],
             cost_estimate=pl.CostEstimate(
                 flops=6 * chunk_rows * rows * width,
                 bytes_accessed=4 * rows * width + 4 * chunk_rows * rows,

time: 337 us -> 335 us (level)
  no operation moved by 1% of the time
where the time goes in v3:
time: 335 us; the launch traced here: 334 us
  waiting for transfers between devices  195 us (58%)
  Pallas kernels  92.2 us (28%)
  other arithmetic  16.3 us (5%)
  between operations  13.3 us (4%)
  starting transfers between devices  11.3 us (3%)
  local copies, waits for them, and re-layouts  5.73 us (2%)
    reduce_scatter x3, waiting for transfers between devices, on_device(): lax.psum_scatter(partial, 'pcol', scatter_dimension=0, tiled=True)  169 us
    pallas_call x3, Pallas kernels, on_device(): pl.pallas_call(product_kernel, grid=(row_blocks,), in_specs=[pl.BlockSpec...  65.2 us
    pallas_call x2, Pallas kernels, on_device(): pl.pallas_call(functools.partial(prep_kernel, begin=first_step * PREP_ROW...  27 us
    ppermute x6, waiting for transfers between devices, broadcast(): landed = lax.ppermute(held, 'prow', moves)  21.9 us
    ppermute x6, starting transfers between devices, broadcast(): landed = lax.ppermute(held, 'prow', moves)  8.7 us
  transfers between devices with their start and end apart: 12, of which 6 were waited for; matrix products, arithmetic and copies ran while one was open for 4% of the time, Pallas kernels for 28%

profile of v3, /device:TPU:0, one launch (start us, length us, event | category | flops | bytes accessed | tf_op | source)
XLA Modules:
  0.0 334.3 jit_solution(12233196329452183235)
XLA Ops:
  6.5 0.0 reduce-scatter.4.cloned.1.call-start
  6.6 0.0 slice-start
  6.6 2.2 slice-done
  8.8 0.7 compare_select_fusion
  9.5 0.0 copy-start
  9.5 1.9 copy-done
  11.4 0.1 slice.17
  11.5 0.7 collective-permute-start
  12.2 0.0 copy-start.1
  12.2 0.0 collective-permute-done
  12.2 1.0 broadcast_select_fusion.8
  13.2 1.4 collective-permute-start.1
  14.6 1.4 slice.18
  16.0 1.8 collective-permute-start.3
  17.8 0.0 copy-done.1
  17.8 0.1 slice.19
  17.9 0.0 copy-start.2
  17.9 2.1 collective-permute-start.6
  20.0 0.6 pad_add_fusion.place
  20.6 13.2 %shard_map.17 = (bf16[3072,2048]{1,0:T(8,128)(2,1)}, bf16[3072,2048]{1,0:T(8,128)(2,1)}) custom-call(s32[2]{0:T(128)} %pad_add_fusion.place, f32[49152,128]{1,0:T(8,128)} %bitcast.11), custom_call_target="tpu_custom_call" | custom-call | flops 62914560 | bytes 25165824 | tf_op jit(solution)/shard_map/pallas_call | solution.py:156
  33.8 0.0 copy-done.2
  33.8 13.8 %shard_map.18 = (bf16[3072,2048]{1,0:T(8,128)(2,1)}, bf16[3072,2048]{1,0:T(8,128)(2,1)}) custom-call(s32[2]{0:T(128)} %pad_add_fusion.place, f32[49152,128]{1,0:T(8,128)} %bitcast.12, bf16[3072,2048]{1,0:T(8,128)(2,1)} %get-tuple-element.9.refs_0_, bf16[3072,2048]{1,0:T(8,128)(2,1)} %get-tuple-element.10.refs_1_), custom_call_target="tpu_custom_call", output_to_operand_aliasing={{0}: (2, {}), {1}: (3, {})} | custom-call | flops 62914560 | bytes 25165824 | tf_op jit(solution)/shard_map/pallas_call | solution.py:156
  47.6 0.0 collective-permute-done.1
  47.6 1.2 broadcast_select_fusion.9
  48.9 0.6 collective-permute-start.2
  49.4 0.0 collective-permute-done.3
  49.4 1.4 broadcast_select_fusion.4
  50.8 1.3 collective-permute-start.4
  52.1 0.0 collective-permute-done.2
  52.1 1.3 broadcast_select_fusion.10
  53.4 16.1 %shard_map.19 = f32[4608,128]{1,0:T(8,128)} custom-call(f32[1536,128]{1,0:T(8,128)} %get-tuple-element.18.first, f32[1536,128]{1,0:T(8,128)} %get-tuple-element.17.second, bf16[3072,2048]{1,0:T(8,128)(2,1)} %get-tuple-element.11.high_ref, bf16[3072,2048]{1,0:T(8,128)(2,1)} %get-tuple-element.12.low_ref), custom_call_target="tpu_custom_call" | custom-call | flops 7247757312 | bytes 27525120 | tf_op jit(solution)/shard_map/pallas_call | solution.py:186
  69.4 0.0 reduce-scatter.4.cloned.1.call-update
  69.5 0.0 reduce-scatter.6.cloned.1.call-start
  69.5 0.0 copy-start.3
  69.5 14.7 %collective-permute-done.4 = f32[2560,128]{1,0:T(8,128)S(1)} collective-permute-done((f32[2560,128]{1,0:T(8,128)}, f32[2560,128]{1,0:T(8,128)S(1)}, u32[]{:S(2)}, u32[]{:S(2)}) %collective-permute-start.4) | collective-permute-done | bytes 1310752 | tf_op jit(solution)/shard_map/ppermute | solution.py:107
  84.3 0.1 broadcast_select_fusion.5
  84.4 0.1 collective-permute-start.5
  84.5 0.0 collective-permute-done.6
  84.5 0.0 copy-done.3
  84.5 0.5 broadcast_select_fusion
  85.0 1.5 collective-permute-start.7
  86.4 1.1 collective-permute-done.5
  87.5 1.7 broadcast_select_fusion.6
  89.2 19.8 %shard_map.20 = f32[7680,128]{1,0:T(8,128)} custom-call(f32[2560,128]{1,0:T(8,128)} %get-tuple-element.16.first, f32[2560,128]{1,0:T(8,128)} %get-tuple-element.15.second, bf16[3072,2048]{1,0:T(8,128)(2,1)} %get-tuple-element.11.high_ref, bf16[3072,2048]{1,0:T(8,128)(2,1)} %get-tuple-element.12.low_ref), custom_call_target="tpu_custom_call" | custom-call | flops 12079595520 | bytes 29097984 | tf_op jit(solution)/shard_map/pallas_call | solution.py:186
  109.1 0.0 reduce-scatter.6.cloned.1.call-update
  109.1 0.0 reduce-scatter.8.cloned.1.call-start
  109.2 7.2 %collective-permute-done.7 = f32[4096,128]{1,0:T(8,128)} collective-permute-done((f32[4096,128]{1,0:T(8,128)S(1)}, f32[4096,128]{1,0:T(8,128)}, u32[]{:S(2)}, u32[]{:S(2)}) %collective-permute-start.7) | collective-permute-done | bytes 2097184 | tf_op jit(solution)/shard_map/ppermute | solution.py:107
  116.3 1.8 broadcast_select_fusion.1
  118.2 1.9 collective-permute-start.8
  120.1 3.8 %collective-permute-done.8 = f32[4096,128]{1,0:T(8,128)S(1)} collective-permute-done((f32[4096,128]{1,0:T(8,128)S(1)}, f32[4096,128]{1,0:T(8,128)S(1)}, u32[]{:S(2)}, u32[]{:S(2)}) %collective-permute-start.8) | collective-permute-done | bytes 2097184 | tf_op jit(solution)/shard_map/ppermute | solution.py:110
  123.9 2.2 broadcast_select_fusion.2
  126.1 29.3 %shard_map.21 = f32[12288,128]{1,0:T(8,128)} custom-call(f32[4096,128]{1,0:T(8,128)} %get-tuple-element.14.first, f32[4096,128]{1,0:T(8,128)} %get-tuple-element.13.second, bf16[3072,2048]{1,0:T(8,128)(2,1)} %get-tuple-element.11.high_ref, bf16[3072,2048]{1,0:T(8,128)(2,1)} %get-tuple-element.12.low_ref), custom_call_target="tpu_custom_call" | custom-call | flops 19327352832 | bytes 31457280 | tf_op jit(solution)/shard_map/pallas_call | solution.py:186
  155.4 0.0 reduce-scatter.8.cloned.1.call-update
  155.4 0.0 reduce-scatter.4.cloned.1.call-done
  155.5 55.0 %reduce-scatter.6.cloned.1.call-done = f32[1920,128]{1,0:T(8,128)} async-done(((f32[7680,128]{1,0:T(8,128)}), f32[1920,128]{1,0:T(8,128)}) %reduce-scatter.6.cloned.1.call-update) | async-done | bytes 983056 | tf_op jit(solution)/shard_map/reduce_scatter | solution.py:200
  210.5 113.6 %reduce-scatter.8.cloned.1.call-done = f32[3072,128]{1,0:T(8,128)} async-done(((f32[12288,128]{1,0:T(8,128)}), f32[3072,128]{1,0:T(8,128)}) %reduce-scatter.8.cloned.1.call-update) | async-done | bytes 1572880 | tf_op jit(solution)/shard_map/reduce_scatter | solution.py:200
  324.0 3.7 %pad_maximum_fusion = f32[6144,128]{1,0:T(8,128)} fusion(f32[3072,128]{1,0:T(8,128)} %reduce-scatter.8.cloned.1.call-done, f32[1920,128]{1,0:T(8,128)} %reduce-scatter.6.cloned.1.call-done, f32[1152,128]{1,0:T(8,128)} %reduce-scatter.4.cloned.1.call-done), kind=kLoop, calls=%fused_computation.1 | loop fusion | flops 1572864 | bytes 6291456 | tf_op jit(solution)/shard_map/concatenate | solution.py:201
  (2 shorter events, 0.0 us)
Async XLA Ops:
  6.5 148.9 %reduce-scatter.4.cloned.1.call-start = ((), (), s32[]{:S(2)}) async-start(), calls=%async_computation.3 | async-start | bytes 2949120 | tf_op jit(solution)/shard_map/reduce_scatter | solution.py:200
  6.6 2.2 slice-start
  9.5 1.9 copy-start
  11.5 0.7 collective-permute-start
  12.2 5.6 %copy-start.1 = (f32[2,256,16,128]{3,2,1,0:T(8,128)S(1)}, f32[2,256,16,128]{3,2,1,0:T(8,128)}, u32[]{:S(2)}) copy-start(f32[2,256,16,128]{3,2,1,0:T(8,128)} %copy-done) | copy-start | bytes 12582916
  13.2 34.5 %collective-permute-start.1 = (f32[1536,128]{1,0:T(8,128)}, f32[1536,128]{1,0:T(8,128)}, u32[]{:S(2)}, u32[]{:S(2)}) collective-permute-start(f32[1536,128]{1,0:T(8,128)} %broadcast_select_fusion.8), channel_id=1, source_target_pairs={{24,8},{16,0},{28,20},{12,4},{25,9},{17,1},{29,21},{13,5},{26,10},... | collective-permute-start | bytes 2359304 | tf_op jit(solution)/shard_map/ppermute | solution.py:107
  16.0 33.4 %collective-permute-start.3 = (f32[2560,128]{1,0:T(8,128)S(1)}, f32[2560,128]{1,0:T(8,128)}, u32[]{:S(2)}, u32[]{:S(2)}) collective-permute-start(f32[2560,128]{1,0:T(8,128)S(1)} %bitcast.15), channel_id=1, source_target_pairs={{24,16},{28,12},{25,17},{29,13},{26,18},{30,14},{27,19},{31,15}} | collective-permute-start | bytes 3932168 | tf_op jit(solution)/shard_map/ppermute | solution.py:107
  17.9 15.9 %copy-start.2 = (f32[2,128,16,128]{3,2,1,0:T(8,128)}, f32[2,128,16,128]{3,2,1,0:T(8,128)S(1)}, u32[]{:S(2)}) copy-start(f32[2,128,16,128]{3,2,1,0:T(8,128)S(1)} %slice.19) | copy-start | bytes 6291460
  17.9 66.5 %collective-permute-start.6 = (f32[4096,128]{1,0:T(8,128)S(1)}, f32[4096,128]{1,0:T(8,128)}, u32[]{:S(2)}, u32[]{:S(2)}) collective-permute-start(f32[4096,128]{1,0:T(8,128)S(1)} %bitcast.14), channel_id=1, source_target_pairs={{24,16},{28,12},{25,17},{29,13},{26,18},{30,14},{27,19},{31,15}} | collective-permute-start | bytes 6291464 | tf_op jit(solution)/shard_map/ppermute | solution.py:107
  48.9 3.2 collective-permute-start.2
  50.8 33.5 %collective-permute-start.4 = (f32[2560,128]{1,0:T(8,128)}, f32[2560,128]{1,0:T(8,128)S(1)}, u32[]{:S(2)}, u32[]{:S(2)}) collective-permute-start(f32[2560,128]{1,0:T(8,128)} %broadcast_select_fusion.4), channel_id=1, source_target_pairs={{24,8},{16,0},{28,20},{12,4},{25,9},{17,1},{29,21},{13,5},{26,10},... | collective-permute-start | bytes 3932168 | tf_op jit(solution)/shard_map/ppermute | solution.py:107
  69.5 141.0 %reduce-scatter.6.cloned.1.call-start = ((), (), s32[]{:S(2)}) async-start(), calls=%async_computation.4 | async-start | bytes 4915200 | tf_op jit(solution)/shard_map/reduce_scatter | solution.py:200
  69.5 15.0 %copy-start.3 = (f32[2,128,16,128]{3,2,1,0:T(8,128)S(1)}, f32[2,128,16,128]{3,2,1,0:T(8,128)}, u32[]{:S(2)}) copy-start(f32[2,128,16,128]{3,2,1,0:T(8,128)} %copy-done.2) | copy-start | bytes 6291460
  84.4 3.1 collective-permute-start.5
  85.0 31.4 %collective-permute-start.7 = (f32[4096,128]{1,0:T(8,128)S(1)}, f32[4096,128]{1,0:T(8,128)}, u32[]{:S(2)}, u32[]{:S(2)}) collective-permute-start(f32[4096,128]{1,0:T(8,128)S(1)} %broadcast_select_fusion), channel_id=1, source_target_pairs={{24,8},{16,0},{28,20},{12,4},{25,9},{17,1},{29,21},{13,5},{26,10},... | collective-permute-start | bytes 6291464 | tf_op jit(solution)/shard_map/ppermute | solution.py:107
  109.1 214.9 %reduce-scatter.8.cloned.1.call-start = ((), (), s32[]{:S(2)}) async-start(), calls=%async_computation.5 | async-start | bytes 7864320 | tf_op jit(solution)/shard_map/reduce_scatter | solution.py:200
  118.2 5.7 %collective-permute-start.8 = (f32[4096,128]{1,0:T(8,128)S(1)}, f32[4096,128]{1,0:T(8,128)S(1)}, u32[]{:S(2)}, u32[]{:S(2)}) collective-permute-start(f32[4096,128]{1,0:T(8,128)S(1)} %broadcast_select_fusion.1), channel_id=1, source_target_pairs={{0,4},{4,0},{8,12},{12,8},{16,20},{20,16},{24,28},{28,24},{1,5},{5... | collective-permute-start | bytes 6291464 | tf_op jit(solution)/shard_map/ppermute | solution.py:110
Sparse Core Ops, SparseCore 0:
  69.6 66.5 reduce-scatter.3
  138.4 71.9 reduce-scatter.5
  212.8 111.2 reduce-scatter.7
